TPU v7x, 32 devices: a whole 2x2x4 slice. The times are simulated.
32 devices in a mesh: row: 16 (over z, x, core), ch: 2 (over y).
Axes of the slice: x: 2, y: 2, z: 4, core: 2. Of those that a mesh axis runs over, the one named last changes fastest.
Arguments:
- pair_rep: float32 [256, 256, 128], P('row', 'ch'), may hold values from -6 to 6
- residue_mask: int32 [256], replicated, may hold values 0 or 1
- pair_gain: float32 [2, 128], replicated, may hold values from 0.5 to 1.5
- pair_shift: float32 [2, 128], replicated, may hold values from -3 to 3
- panel_weight: bfloat16 [2, 128, 512], replicated, may hold values from -0.5 to 0.5
- panel_bias: float32 [2, 512], replicated, may hold values from -3 to 3
- gate_weight: bfloat16 [2, 128, 128], replicated, may hold values from -0.5 to 0.5
- gate_bias: float32 [2, 128], replicated, may hold values from -3 to 3
- hidden_gain: float32 [2, 128], replicated, may hold values from 0.5 to 1.5
- hidden_shift: float32 [2, 128], replicated, may hold values from -3 to 3
- output_weight: bfloat16 [2, 128, 128], replicated, may hold values from -0.5 to 0.5
- output_bias: float32 [2, 128], replicated, may hold values from -3 to 3
Outputs:
- updated_pair: float32 [256, 256, 128], P('row', 'ch')
All inputs are finite; a program needn't handle non-finite values.
Results may differ from a plain program's by a relative error of at most 0.0039.
Values may be sent and summed in bfloat16 or wider, within the bound.
A program may use at most 64 MiB of HBM per device.

v0:
```python
import jax
import jax.numpy as jnp
from jax import lax
from jax.sharding import PartitionSpec as P

PAIR_EPSILON = 1e-05
HIDDEN_EPSILON = 1.0


def layer_norm(values, gain_value, shift_value, along, epsilon):
    center = jnp.mean(values, axis=along, keepdims=True)
    offset = values - center
    spread = jnp.mean(offset * offset, axis=along, keepdims=True)
    return offset * lax.rsqrt(spread + epsilon) * gain_value + shift_value


def project(
    current,
    cell_mask,
    section_index,
    pair_gain,
    pair_shift,
    panel_weight,
    panel_bias,
    gate_weight,
    gate_bias,
):
    normed = layer_norm(
        current, pair_gain[section_index], pair_shift[section_index], 2, PAIR_EPSILON
    ).astype(jnp.bfloat16)
    hidden_width = panel_weight.shape[2] // 4
    features = jnp.einsum(
        "rjc,cf->frj", normed, panel_weight[section_index], preferred_element_type=jnp.float32
    )
    features = features + panel_bias[section_index][:, None, None]
    left_panel = (
        cell_mask
        * jax.nn.sigmoid(features[:hidden_width])
        * features[hidden_width : 2 * hidden_width]
    ).astype(jnp.bfloat16)
    right_panel = (
        cell_mask
        * jax.nn.sigmoid(features[2 * hidden_width : 3 * hidden_width])
        * features[3 * hidden_width :]
    ).astype(jnp.bfloat16)
    gate_value = jax.nn.sigmoid(
        jnp.einsum(
            "rjc,cd->rjd", normed, gate_weight[section_index], preferred_element_type=jnp.float32
        )
        + gate_bias[section_index]
    )
    return (left_panel, right_panel, gate_value)


def local(
    pair_rep,
    residue_mask,
    pair_gain,
    pair_shift,
    panel_weight,
    panel_bias,
    gate_weight,
    gate_bias,
    hidden_gain,
    hidden_shift,
    output_weight,
    output_bias,
):
    row_count = pair_rep.shape[0]
    col_count = pair_rep.shape[1]
    hidden_width = panel_weight.shape[2] // 4
    row_total = lax.axis_size("row")
    col_total = lax.axis_size("ch")
    group = hidden_width // col_total
    if group >= row_total:
        per_slot = group // row_total
        quarters = 1
    else:
        per_slot = 1
        quarters = row_total // group
    slots = row_total // quarters
    sub_rows = row_count // quarters
    blocks = col_count // row_count
    row_index = lax.axis_index("row")
    col_index = lax.axis_index("ch")
    residue_float = residue_mask.astype(jnp.float32)
    row_mask = lax.dynamic_slice_in_dim(residue_float, row_index * row_count, row_count)
    col_mask = lax.dynamic_slice_in_dim(residue_float, col_index * col_count, col_count)
    cell_mask = row_mask[:, None] * col_mask[None, :]
    current = pair_rep
    for section_index in range(2):
        left_panel, right_panel, gate_value = project(
            current,
            cell_mask,
            section_index,
            pair_gain,
            pair_shift,
            panel_weight,
            panel_bias,
            gate_weight,
            gate_bias,
        )
        if section_index == 0:
            send_left = left_panel.reshape(
                col_total, slots, per_slot, quarters, sub_rows, col_count
            )
            send_left = jnp.transpose(send_left, (0, 1, 3, 2, 4, 5)).reshape(
                col_total, row_total, per_slot, sub_rows, col_count
            )
        else:
            send_left = left_panel.reshape(
                col_total, slots, per_slot, row_count, blocks, quarters, sub_rows
            )
            send_left = jnp.transpose(send_left, (0, 1, 5, 2, 3, 4, 6)).reshape(
                col_total, row_total, per_slot, row_count, blocks * sub_rows
            )
        send_right = right_panel.reshape(col_total, slots, 1, per_slot, row_count, col_count)
        send_right = jnp.broadcast_to(
            send_right, (col_total, slots, quarters, per_slot, row_count, col_count)
        ).reshape(col_total, row_total, per_slot, row_count, col_count)
        got_left, got_right = (
            lax.all_to_all(
                lax.all_to_all(send_left, "ch", split_axis=0, concat_axis=4, tiled=True),
                "row",
                split_axis=1,
                concat_axis=3,
                tiled=True,
            ),
            lax.all_to_all(
                lax.all_to_all(send_right, "ch", split_axis=0, concat_axis=4, tiled=True),
                "row",
                split_axis=1,
                concat_axis=3,
                tiled=True,
            ),
        )
        got_left = got_left[0, 0]
        got_right = got_right[0, 0]
        if section_index == 0:
            products = jnp.einsum(
                "hik,hjk->hij", got_left, got_right, preferred_element_type=jnp.float32
            )
        else:
            products = jnp.einsum(
                "hki,hkj->hij", got_left, got_right, preferred_element_type=jnp.float32
            )
        returned = products.reshape(per_slot, row_total, sub_rows, col_total, col_count)
        gathered = lax.all_to_all(
            lax.all_to_all(returned, "row", split_axis=1, concat_axis=0, tiled=True),
            "ch",
            split_axis=3,
            concat_axis=0,
            tiled=True,
        )
        gathered = gathered.reshape(col_total, slots, quarters, per_slot, sub_rows, col_count)
        gathered = jnp.transpose(gathered, (0, 1, 3, 2, 4, 5)).reshape(
            hidden_width, row_count, col_count
        )
        normed = layer_norm(
            gathered,
            hidden_gain[section_index][:, None, None],
            hidden_shift[section_index][:, None, None],
            0,
            HIDDEN_EPSILON,
        ).astype(jnp.bfloat16)
        projected = jnp.einsum(
            "hrj,hc->rjc", normed, output_weight[section_index], preferred_element_type=jnp.float32
        )
        current = current + gate_value * (projected + output_bias[section_index])
    return current


def solution(mesh):
    return jax.shard_map(
        local,
        mesh=mesh,
        in_specs=(P("row", "ch", None), P(), P(), P(), P(), P(), P(), P(), P(), P(), P(), P()),
        out_specs=P("row", "ch", None),
        check_vma=False,
    )
```

profile of v0, /device:TPU:0, one launch (start us, length us, event | category | flops | bytes accessed | tf_op | source)
XLA Modules:
  0.0 238.2 jit_solution(15132575258035576822)
XLA Ops:
  0.8 1.6 reduce_sum.72
  2.4 1.9 multiply_reduce_fusion.3
  6.7 2.1 add_bitcast_fusion.1
  9.4 1.2 copy.82
  10.6 4.3 %all-to-all-start = ((bf16[2,16,4,16,128]{4,3,2,1,0:T(8,128)(2,1)}), bf16[2,16,4,16,128]{4,3,2,1,0:T(8,128)(2,1)S(1)}, u32[]{:S(2)}, u32[]{:S(2)}) async-start(bf16[2,16,4,16,128]{4,3,2,1,0:T(8,128)(2,1)} %bitcast.9), calls=%async_computation | async-start | bytes 1048576 | tf_op jit(solution)/shard_map/all_to_all | solution.py:123
  14.9 1.2 copy.86
  16.0 7.5 %all-to-all-done = bf16[2,16,4,16,128]{4,3,2,1,0:T(8,128)(2,1)S(1)} async-done(((bf16[2,16,4,16,128]{4,3,2,1,0:T(8,128)(2,1)}), bf16[2,16,4,16,128]{4,3,2,1,0:T(8,128)(2,1)S(1)}, u32[]{:S(2)}, u32[]{:S(2)}) %all-to-all-start) | async-done | bytes 524320 | tf_op jit(solution)/shard_map/all_to_all | solution.py:123
  23.6 3.5 %all-to-all-start.2 = ((bf16[2,16,4,16,128]{4,3,2,1,0:T(8,128)(2,1)}), bf16[2,16,4,16,128]{4,3,2,1,0:T(8,128)(2,1)S(1)}, u32[]{:S(2)}, u32[]{:S(2)}) async-start(bf16[2,16,4,16,128]{4,3,2,1,0:T(8,128)(2,1)} %bitcast.16), calls=%async_computation.2 | async-start | bytes 1048576 | tf_op jit(solution)/shard_map/all_to_all | solution.py:130
  28.0 6.8 %all-to-all-done.2 = bf16[2,16,4,16,128]{4,3,2,1,0:T(8,128)(2,1)S(1)} async-done(((bf16[2,16,4,16,128]{4,3,2,1,0:T(8,128)(2,1)}), bf16[2,16,4,16,128]{4,3,2,1,0:T(8,128)(2,1)S(1)}, u32[]{:S(2)}, u32[]{:S(2)}) %all-to-all-start.2) | async-done | bytes 524320 | tf_op jit(solution)/shard_map/all_to_all | solution.py:130
  34.7 5.9 %all-to-all-start.1 = ((bf16[1,16,4,16,256]{4,3,2,0,1:T(8,128)(2,1)}), bf16[1,16,4,16,256]{4,3,2,0,1:T(8,128)(2,1)S(1)}, u32[]{:S(2)}, u32[]{:S(2)}) async-start(bf16[1,16,4,16,256]{4,3,2,0,1:T(8,128)(2,1)} %bitcast_bitcast_fusion.3), calls=%async_computation.1 | async-start | bytes 1048576 | tf_op jit(solution)/shard_map/all_to_all | solution.py:122
  41.5 13.4 %all-to-all-done.1 = bf16[1,16,4,16,256]{4,3,2,0,1:T(8,128)(2,1)S(1)} async-done(((bf16[1,16,4,16,256]{4,3,2,0,1:T(8,128)(2,1)}), bf16[1,16,4,16,256]{4,3,2,0,1:T(8,128)(2,1)S(1)}, u32[]{:S(2)}, u32[]{:S(2)}) %all-to-all-start.1) | async-done | bytes 524320 | tf_op jit(solution)/shard_map/all_to_all | solution.py:122
  54.9 4.2 %all-to-all-start.3 = ((bf16[1,16,4,16,256]{4,3,2,0,1:T(8,128)(2,1)}), bf16[1,16,4,16,256]{4,3,2,0,1:T(8,128)(2,1)S(1)}, u32[]{:S(2)}, u32[]{:S(2)}) async-start(bf16[1,16,4,16,256]{4,3,2,0,1:T(8,128)(2,1)} %bitcast_bitcast_fusion.2), calls=%async_computation.3 | async-start | bytes 1048576 | tf_op jit(solution)/shard_map/all_to_all | solution.py:129
  59.1 14.2 %all-to-all-done.3 = bf16[1,16,4,16,256]{4,3,2,0,1:T(8,128)(2,1)S(1)} async-done(((bf16[1,16,4,16,256]{4,3,2,0,1:T(8,128)(2,1)}), bf16[1,16,4,16,256]{4,3,2,0,1:T(8,128)(2,1)S(1)}, u32[]{:S(2)}, u32[]{:S(2)}) %all-to-all-start.3) | async-done | bytes 524320 | tf_op jit(solution)/shard_map/all_to_all | solution.py:129
  74.4 28.8 %all_to_all.198 = f32[4,16,16,2,128]{4,2,3,0,1:T(8,128)S(1)} all-to-all(f32[4,16,16,2,128]{4,2,3,0,1:T(8,128)S(1)} %copy.90), channel_id=1, replica_groups=mesh['row'=16,'ch'=2] {'row'}, dimensions={1} | all-to-all | bytes 2097152 | tf_op jit(solution)/shard_map/all_to_all | solution.py:149
  103.2 1.1 copy.91
  104.3 3.6 %all-to-all-start.5 = ((f32[64,1,16,2,128]{4,2,1,0,3:T(8,128)}), f32[64,1,16,2,128]{4,2,1,0,3:T(8,128)S(1)}, u32[]{:S(2)}, u32[]{:S(2)}) async-start(f32[64,1,16,2,128]{4,2,1,0,3:T(8,128)} %copy.91), calls=%async_computation.5 | async-start | bytes 2097152 | tf_op jit(solution)/shard_map/all_to_all | solution.py:148
  108.4 2.0 fusion.11
  110.4 12.4 %all-to-all-done.5 = f32[64,1,16,2,128]{4,2,1,0,3:T(8,128)S(1)} async-done(((f32[64,1,16,2,128]{4,2,1,0,3:T(8,128)}), f32[64,1,16,2,128]{4,2,1,0,3:T(8,128)S(1)}, u32[]{:S(2)}, u32[]{:S(2)}) %all-to-all-start.5) | async-done | bytes 1048608 | tf_op jit(solution)/shard_map/all_to_all | solution.py:148
  126.0 1.2 copy.102
  127.2 3.5 %all-to-all-start.8 = ((bf16[2,16,4,16,128]{4,3,2,1,0:T(8,128)(2,1)}), bf16[2,16,4,16,128]{4,3,2,1,0:T(8,128)(2,1)S(1)}, u32[]{:S(2)}, u32[]{:S(2)}) async-start(bf16[2,16,4,16,128]{4,3,2,1,0:T(8,128)(2,1)} %bitcast.49), calls=%async_computation.8 | async-start | bytes 1048576 | tf_op jit(solution)/shard_map/all_to_all | solution.py:130
  130.7 1.2 copy.98
  131.9 7.3 %all-to-all-done.8 = bf16[2,16,4,16,128]{4,3,2,1,0:T(8,128)(2,1)S(1)} async-done(((bf16[2,16,4,16,128]{4,3,2,1,0:T(8,128)(2,1)}), bf16[2,16,4,16,128]{4,3,2,1,0:T(8,128)(2,1)S(1)}, u32[]{:S(2)}, u32[]{:S(2)}) %all-to-all-start.8) | async-done | bytes 524320 | tf_op jit(solution)/shard_map/all_to_all | solution.py:130
  139.2 3.5 %all-to-all-start.6 = ((bf16[2,16,4,16,128]{4,3,2,1,0:T(8,128)(2,1)}), bf16[2,16,4,16,128]{4,3,2,1,0:T(8,128)(2,1)S(1)}, u32[]{:S(2)}, u32[]{:S(2)}) async-start(bf16[2,16,4,16,128]{4,3,2,1,0:T(8,128)(2,1)} %bitcast.42), calls=%async_computation.6 | async-start | bytes 1048576 | tf_op jit(solution)/shard_map/all_to_all | solution.py:123
  143.6 6.8 %all-to-all-done.6 = bf16[2,16,4,16,128]{4,3,2,1,0:T(8,128)(2,1)S(1)} async-done(((bf16[2,16,4,16,128]{4,3,2,1,0:T(8,128)(2,1)}), bf16[2,16,4,16,128]{4,3,2,1,0:T(8,128)(2,1)S(1)}, u32[]{:S(2)}, u32[]{:S(2)}) %all-to-all-start.6) | async-done | bytes 524320 | tf_op jit(solution)/shard_map/all_to_all | solution.py:123
  150.4 3.6 %all-to-all-start.9 = ((bf16[1,16,4,16,256]{4,3,2,0,1:T(8,128)(2,1)}), bf16[1,16,4,16,256]{4,3,2,0,1:T(8,128)(2,1)S(1)}, u32[]{:S(2)}, u32[]{:S(2)}) async-start(bf16[1,16,4,16,256]{4,3,2,0,1:T(8,128)(2,1)} %bitcast_bitcast_fusion), calls=%async_computation.9 | async-start | bytes 1048576 | tf_op jit(solution)/shard_map/all_to_all | solution.py:129
  154.8 13.4 %all-to-all-done.9 = bf16[1,16,4,16,256]{4,3,2,0,1:T(8,128)(2,1)S(1)} async-done(((bf16[1,16,4,16,256]{4,3,2,0,1:T(8,128)(2,1)}), bf16[1,16,4,16,256]{4,3,2,0,1:T(8,128)(2,1)S(1)}, u32[]{:S(2)}, u32[]{:S(2)}) %all-to-all-start.9) | async-done | bytes 524320 | tf_op jit(solution)/shard_map/all_to_all | solution.py:129
  168.2 4.1 %all-to-all-start.7 = ((bf16[1,16,4,16,256]{4,3,2,0,1:T(8,128)(2,1)}), bf16[1,16,4,16,256]{4,3,2,0,1:T(8,128)(2,1)S(1)}, u32[]{:S(2)}, u32[]{:S(2)}) async-start(bf16[1,16,4,16,256]{4,3,2,0,1:T(8,128)(2,1)} %bitcast_bitcast_fusion.1), calls=%async_computation.7 | async-start | bytes 1048576 | tf_op jit(solution)/shard_map/all_to_all | solution.py:122
  172.3 14.2 %all-to-all-done.7 = bf16[1,16,4,16,256]{4,3,2,0,1:T(8,128)(2,1)S(1)} async-done(((bf16[1,16,4,16,256]{4,3,2,0,1:T(8,128)(2,1)}), bf16[1,16,4,16,256]{4,3,2,0,1:T(8,128)(2,1)S(1)}, u32[]{:S(2)}, u32[]{:S(2)}) %all-to-all-start.7) | async-done | bytes 524320 | tf_op jit(solution)/shard_map/all_to_all | solution.py:122
  187.6 28.6 %all_to_all.199 = f32[4,16,16,2,128]{4,2,3,0,1:T(8,128)S(1)} all-to-all(f32[4,16,16,2,128]{4,2,3,0,1:T(8,128)S(1)} %copy.107), channel_id=1, replica_groups=mesh['row'=16,'ch'=2] {'row'}, dimensions={1} | all-to-all | bytes 2097152 | tf_op jit(solution)/shard_map/all_to_all | solution.py:149
  217.3 3.6 %all-to-all-start.11 = ((f32[64,1,16,2,128]{4,2,1,0,3:T(8,128)}), f32[64,1,16,2,128]{4,2,1,0,3:T(8,128)S(1)}, u32[]{:S(2)}, u32[]{:S(2)}) async-start(f32[64,1,16,2,128]{4,2,1,0,3:T(8,128)} %copy.108), calls=%async_computation.11 | async-start | bytes 2097152 | tf_op jit(solution)/shard_map/all_to_all | solution.py:148
  221.6 14.3 %all-to-all-done.11 = f32[64,1,16,2,128]{4,2,1,0,3:T(8,128)S(1)} async-done(((f32[64,1,16,2,128]{4,2,1,0,3:T(8,128)}), f32[64,1,16,2,128]{4,2,1,0,3:T(8,128)S(1)}, u32[]{:S(2)}, u32[]{:S(2)}) %all-to-all-start.11) | async-done | bytes 1048608 | tf_op jit(solution)/shard_map/all_to_all | solution.py:148
  236.9 1.3 copy.111
  (68 shorter events, 15.8 us)
Async XLA Ops:
  10.6 13.0 %all-to-all-start = ((bf16[2,16,4,16,128]{4,3,2,1,0:T(8,128)(2,1)}), bf16[2,16,4,16,128]{4,3,2,1,0:T(8,128)(2,1)S(1)}, u32[]{:S(2)}, u32[]{:S(2)}) async-start(bf16[2,16,4,16,128]{4,3,2,1,0:T(8,128)(2,1)} %bitcast.9), calls=%async_computation | async-start | bytes 1048576 | tf_op jit(solution)/shard_map/all_to_all | solution.py:123
  23.6 11.2 %all-to-all-start.2 = ((bf16[2,16,4,16,128]{4,3,2,1,0:T(8,128)(2,1)}), bf16[2,16,4,16,128]{4,3,2,1,0:T(8,128)(2,1)S(1)}, u32[]{:S(2)}, u32[]{:S(2)}) async-start(bf16[2,16,4,16,128]{4,3,2,1,0:T(8,128)(2,1)} %bitcast.16), calls=%async_computation.2 | async-start | bytes 1048576 | tf_op jit(solution)/shard_map/all_to_all | solution.py:130
  34.7 20.1 %all-to-all-start.1 = ((bf16[1,16,4,16,256]{4,3,2,0,1:T(8,128)(2,1)}), bf16[1,16,4,16,256]{4,3,2,0,1:T(8,128)(2,1)S(1)}, u32[]{:S(2)}, u32[]{:S(2)}) async-start(bf16[1,16,4,16,256]{4,3,2,0,1:T(8,128)(2,1)} %bitcast_bitcast_fusion.3), calls=%async_computation.1 | async-start | bytes 1048576 | tf_op jit(solution)/shard_map/all_to_all | solution.py:122
  54.9 18.4 %all-to-all-start.3 = ((bf16[1,16,4,16,256]{4,3,2,0,1:T(8,128)(2,1)}), bf16[1,16,4,16,256]{4,3,2,0,1:T(8,128)(2,1)S(1)}, u32[]{:S(2)}, u32[]{:S(2)}) async-start(bf16[1,16,4,16,256]{4,3,2,0,1:T(8,128)(2,1)} %bitcast_bitcast_fusion.2), calls=%async_computation.3 | async-start | bytes 1048576 | tf_op jit(solution)/shard_map/all_to_all | solution.py:129
  74.3 33.6 %copy-start.5 = (f32[2,128]{1,0:T(2,128)S(1)}, f32[2,128]{1,0:T(2,128)}, u32[]{:S(2)}) copy-start(f32[2,128]{1,0:T(2,128)} %param.21) | copy-start | bytes 3076
  74.3 33.6 %copy-start.6 = (f32[2,128]{1,0:T(2,128)S(1)}, f32[2,128]{1,0:T(2,128)}, u32[]{:S(2)}) copy-start(f32[2,128]{1,0:T(2,128)} %param.20) | copy-start | bytes 3076
  74.3 33.6 %copy-start = (f32[16,128,128]{2,1,0:T(8,128)S(1)}, f32[16,128,128]{2,1,0:T(8,128)}, u32[]{:S(2)}) copy-start(f32[16,128,128]{2,1,0:T(8,128)} %param.12) | copy-start | bytes 3145732
  74.4 34.0 %copy-start.4 = (f32[2,128]{1,0:T(2,128)S(1)}, f32[2,128]{1,0:T(2,128)}, u32[]{:S(2)}) copy-start(f32[2,128]{1,0:T(2,128)} %param.23) | copy-start | bytes 3076
  74.4 34.0 %copy-start.7 = (bf16[2,128,128]{2,1,0:T(8,128)(2,1)S(1)}, bf16[2,128,128]{2,1,0:T(8,128)(2,1)}, u32[]{:S(2)}) copy-start(bf16[2,128,128]{2,1,0:T(8,128)(2,1)} %param.18) | copy-start | bytes 196612
  104.3 18.6 %all-to-all-start.5 = ((f32[64,1,16,2,128]{4,2,1,0,3:T(8,128)}), f32[64,1,16,2,128]{4,2,1,0,3:T(8,128)S(1)}, u32[]{:S(2)}, u32[]{:S(2)}) async-start(f32[64,1,16,2,128]{4,2,1,0,3:T(8,128)} %copy.91), calls=%async_computation.5 | async-start | bytes 2097152 | tf_op jit(solution)/shard_map/all_to_all | solution.py:148
  108.4 15.1 %copy-start.3 = (bf16[2,128,128]{2,1,0:T(8,128)(2,1)S(1)}, bf16[2,128,128]{2,1,0:T(8,128)(2,1)}, u32[]{:S(2)}) copy-start(bf16[2,128,128]{2,1,0:T(8,128)(2,1)} %param.22) | copy-start | bytes 196612
  110.4 14.1 %copy-start.2 = (bf16[2,128,512]{2,1,0:T(8,128)(2,1)S(1)}, bf16[2,128,512]{2,1,0:T(8,128)(2,1)}, u32[]{:S(2)}) copy-start(bf16[2,128,512]{2,1,0:T(8,128)(2,1)} %param.16) | copy-start | bytes 786436
  122.8 1.2 copy-start.1
  127.2 12.0 %all-to-all-start.8 = ((bf16[2,16,4,16,128]{4,3,2,1,0:T(8,128)(2,1)}), bf16[2,16,4,16,128]{4,3,2,1,0:T(8,128)(2,1)S(1)}, u32[]{:S(2)}, u32[]{:S(2)}) async-start(bf16[2,16,4,16,128]{4,3,2,1,0:T(8,128)(2,1)} %bitcast.49), calls=%async_computation.8 | async-start | bytes 1048576 | tf_op jit(solution)/shard_map/all_to_all | solution.py:130
  139.2 11.2 %all-to-all-start.6 = ((bf16[2,16,4,16,128]{4,3,2,1,0:T(8,128)(2,1)}), bf16[2,16,4,16,128]{4,3,2,1,0:T(8,128)(2,1)S(1)}, u32[]{:S(2)}, u32[]{:S(2)}) async-start(bf16[2,16,4,16,128]{4,3,2,1,0:T(8,128)(2,1)} %bitcast.42), calls=%async_computation.6 | async-start | bytes 1048576 | tf_op jit(solution)/shard_map/all_to_all | solution.py:123
  150.4 17.8 %all-to-all-start.9 = ((bf16[1,16,4,16,256]{4,3,2,0,1:T(8,128)(2,1)}), bf16[1,16,4,16,256]{4,3,2,0,1:T(8,128)(2,1)S(1)}, u32[]{:S(2)}, u32[]{:S(2)}) async-start(bf16[1,16,4,16,256]{4,3,2,0,1:T(8,128)(2,1)} %bitcast_bitcast_fusion), calls=%async_computation.9 | async-start | bytes 1048576 | tf_op jit(solution)/shard_map/all_to_all | solution.py:129
  168.2 18.4 %all-to-all-start.7 = ((bf16[1,16,4,16,256]{4,3,2,0,1:T(8,128)(2,1)}), bf16[1,16,4,16,256]{4,3,2,0,1:T(8,128)(2,1)S(1)}, u32[]{:S(2)}, u32[]{:S(2)}) async-start(bf16[1,16,4,16,256]{4,3,2,0,1:T(8,128)(2,1)} %bitcast_bitcast_fusion.1), calls=%async_computation.7 | async-start | bytes 1048576 | tf_op jit(solution)/shard_map/all_to_all | solution.py:122
  187.5 33.6 %copy-start.8 = (bf16[2,128,128]{2,1,0:T(8,128)(2,1)S(1)}, bf16[2,128,128]{2,1,0:T(8,128)(2,1)}, u32[]{:S(2)}) copy-start(bf16[2,128,128]{2,1,0:T(8,128)(2,1)} %param.18) | copy-start | bytes 196612
  217.3 18.6 %all-to-all-start.11 = ((f32[64,1,16,2,128]{4,2,1,0,3:T(8,128)}), f32[64,1,16,2,128]{4,2,1,0,3:T(8,128)S(1)}, u32[]{:S(2)}, u32[]{:S(2)}) async-start(f32[64,1,16,2,128]{4,2,1,0,3:T(8,128)} %copy.108), calls=%async_computation.11 | async-start | bytes 2097152 | tf_op jit(solution)/shard_map/all_to_all | solution.py:148
where the time goes:
time: 240 us; the launch traced here: 238 us
  waiting for transfers between devices  110 us (46%)
  blocking collectives  57.4 us (24%)
  starting transfers between devices  39.6 us (16%)
  local copies, waits for them, and re-layouts  16.7 us (7%)
  matrix products  6.89 us (3%)
  other arithmetic  6.83 us (3%)
    all_to_all x2, blocking collectives, local(): lax.all_to_all(returned, 'row', split_axis=1, concat_axis=0, tiled=True)  57.4 us
    all_to_all x2, waiting for transfers between devices, local(): lax.all_to_all(lax.all_to_all(send_left, 'ch', split_axis=0, concat_axis=...  27.6 us
    all_to_all x2, waiting for transfers between devices, local(): lax.all_to_all(lax.all_to_all(send_right, 'ch', split_axis=0, concat_axis...  27.6 us
    all_to_all x2, waiting for transfers between devices, local(): lax.all_to_all(lax.all_to_all(returned, 'row', split_axis=1, concat_axis=...  26.7 us
    all_to_all x2, waiting for transfers between devices, local(): lax.all_to_all(send_left, 'ch', split_axis=0, concat_axis=4, tiled=True)  14.4 us
    all_to_all x2, waiting for transfers between devices, local(): lax.all_to_all(send_right, 'ch', split_axis=0, concat_axis=4, tiled=True)  14.1 us
    all_to_all x2, starting transfers between devices, local(): lax.all_to_all(lax.all_to_all(send_left, 'ch', split_axis=0, concat_axis=...  9.96 us
    all_to_all x2, starting transfers between devices, local(): lax.all_to_all(send_left, 'ch', split_axis=0, concat_axis=4, tiled=True)  7.75 us
  transfers between devices with their start and end apart: 10, of which 10 were waited for; matrix products, arithmetic and copies ran while one was open for 4% of the time, Pallas kernels for 0%

commit v1 on v0

v1 whole, which is shorter than its diff:
```python
import functools

import jax
import jax.numpy as jnp
from jax import lax
from jax.experimental import pallas as pl
from jax.experimental.pallas import tpu as pltpu
from jax.sharding import PartitionSpec as P

PAIR_EPSILON = 1e-05
HIDDEN_EPSILON = 1.0
MESH = pl.DeviceIdType.MESH


def kernel(
    sizes,
    pair_ref,
    mask_smem,
    mask_ref,
    pair_gain,
    pair_shift,
    panel_weight,
    panel_bias,
    gate_weight,
    gate_bias,
    hidden_gain,
    hidden_shift,
    output_weight,
    output_bias,
    out_ref,
    weight_t,
    bias_t,
    stage,
    send_ab,
    recv_a,
    recv_b,
    send_x,
    recv_x,
    gate,
    ab_send_sem,
    ab_recv_sem,
    x_send_sem,
    x_recv_sem,
):
    rows, cols, hidden, row_total, col_total, per_slot, quarters = sizes
    devices = row_total * col_total
    group = hidden // col_total
    total = row_total * rows
    part = total // quarters
    my_row = lax.axis_index("row")
    my_col = lax.axis_index("ch")
    me = my_row * col_total + my_col

    def peer_of(step):
        half = (step + 1) // 2
        turn = devices // 2 + half * (1 - 2 * (step % 2)) + devices
        peer = lax.rem(me + turn, devices)
        return peer // col_total, lax.rem(peer, col_total)

    barrier = pltpu.get_barrier_semaphore()

    def greet(step, carry):
        peer_row, peer_col = peer_of(step)
        pl.semaphore_signal(barrier, inc=1, device_id=(peer_row, peer_col), device_id_type=MESH)
        return carry

    lax.fori_loop(0, devices - 1, greet, 0)

    def hidden_offset(row, col):
        return col * group + (row // quarters) * per_slot

    def ab_refs(section, which, row, col):
        source = send_ab.at[section, which, pl.ds(hidden_offset(row, col), per_slot)]
        row_at = pl.multiple_of(my_row * rows, rows)
        col_at = pl.multiple_of(my_col * cols, cols)
        if which == 0:
            if section == 0:
                row_at = pl.multiple_of(lax.rem(row_at, part), rows)
                target = recv_a[0].at[:, pl.ds(row_at, rows), pl.ds(col_at, cols)]
            else:
                col_at = pl.multiple_of(lax.rem(col_at, part), cols)
                target = recv_a[1].at[:, pl.ds(row_at, rows), pl.ds(col_at, cols)]
        else:
            target = recv_b.at[section, :, pl.ds(row_at, rows), pl.ds(col_at, cols)]
        return source, target

    def my_part(section):
        return my_row * rows // part if section == 0 else my_col * cols // part

    def ab_copies(section, step, act):
        peer_row, peer_col = peer_of(step)
        for which in range(2):
            source, target = ab_refs(section, which, peer_row, peer_col)
            copy = pltpu.make_async_remote_copy(
                src_ref=source,
                dst_ref=target,
                send_sem=ab_send_sem.at[section, which],
                recv_sem=ab_recv_sem.at[section, which],
                device_id=(peer_row, peer_col),
                device_id_type=MESH,
            )
            if which == 0 and quarters > 1:
                pl.when(lax.rem(peer_row, quarters) == my_part(section))(functools.partial(act, copy))
            else:
                act(copy)

    def ab_own(section):
        for which in range(2):
            source, target = ab_refs(section, which, my_row, my_col)
            copy = pltpu.make_async_copy(source, target, ab_recv_sem.at[section, which])
            if which == 0 and quarters > 1:
                pl.when(lax.rem(my_row, quarters) == my_part(section))(copy.start)
            else:
                copy.start()

    def x_refs(section, row, col):
        row_at = pl.multiple_of(lax.rem(row * rows, part), rows)
        col_at = pl.multiple_of(col * cols, cols)
        source = send_x.at[section, :, pl.ds(row_at, rows), pl.ds(col_at, cols)]
        target = recv_x.at[section, pl.ds(hidden_offset(my_row, my_col), per_slot)]
        return source, target

    def x_copies(section, step, act):
        peer_row, peer_col = peer_of(step)
        source, target = x_refs(section, peer_row, peer_col)
        copy = pltpu.make_async_remote_copy(
            src_ref=source,
            dst_ref=target,
            send_sem=x_send_sem.at[section],
            recv_sem=x_recv_sem.at[section],
            device_id=(peer_row, peer_col),
            device_id_type=MESH,
        )
        if quarters > 1:
            pl.when(peer_row * rows // part == lax.rem(my_row, quarters))(functools.partial(act, copy))
        else:
            act(copy)

    def x_own(section):
        source, target = x_refs(section, my_row, my_col)
        copy = pltpu.make_async_copy(source, target, x_recv_sem.at[section])
        if quarters > 1:
            pl.when(my_row * rows // part == lax.rem(my_row, quarters))(copy.start)
        else:
            copy.start()

    def every_peer(body):
        def step_body(step, carry):
            body(step)
            return carry

        lax.fori_loop(0, devices - 1, step_body, 0)

    start = lambda copy: copy.start()
    wait_send = lambda copy: copy.wait_send()

    def wait_all(ref, sem):
        pltpu.make_async_copy(ref, ref, sem).wait()

    col_mask = mask_ref[pl.ds(my_col, 1), :].astype(jnp.float32)

    for section in range(2):
        current = pair_ref if section == 0 else out_ref
        weight_t[...] = panel_weight[section].astype(jnp.float32).T.astype(jnp.bfloat16)
        bias_t[...] = jnp.broadcast_to(panel_bias[pl.ds(section, 1), :], (cols, 4 * hidden)).T
        gain_row = pair_gain[pl.ds(section, 1), :]
        shift_row = pair_shift[pl.ds(section, 1), :]

        def project(r, carry):
            values = current[r]
            offset = values - jnp.mean(values, axis=1, keepdims=True)
            spread = jnp.mean(offset * offset, axis=1, keepdims=True)
            normed = offset * lax.rsqrt(spread + PAIR_EPSILON) * gain_row + shift_row
            normed = normed.astype(jnp.bfloat16)
            mask = col_mask * mask_smem[my_row * rows + r].astype(jnp.float32)
            for which in range(2):
                base = 2 * which * hidden
                features = lax.dot_general(
                    weight_t[pl.ds(base, 2 * hidden), :],
                    normed,
                    (((1,), (1,)), ((), ())),
                    preferred_element_type=jnp.float32,
                )
                features = features + bias_t[pl.ds(base, 2 * hidden), :]
                panel = mask * jax.nn.sigmoid(features[:hidden]) * features[hidden:]
                stage[which, pl.ds(r, hidden, stride=rows), :] = panel
            gate[r] = jax.nn.sigmoid(
                jnp.dot(normed, gate_weight[section], preferred_element_type=jnp.float32)
                + gate_bias[pl.ds(section, 1), :]
            )
            return carry

        lax.fori_loop(0, rows, project, 0)
        for which in range(2):
            send_ab[section, which] = (
                stage[which].astype(jnp.bfloat16).reshape(hidden, rows, cols)
            )
        if section == 0:
            pl.semaphore_wait(barrier, devices - 1)
        every_peer(lambda step: ab_copies(section, step, start))
        ab_own(section)
        wait_all(recv_a[section], ab_recv_sem.at[section, 0])
        wait_all(recv_b.at[section], ab_recv_sem.at[section, 1])
        for h in range(per_slot):
            left, right = recv_a[section][h], recv_b[section, h]
            contract = 1 if section == 0 else 0
            send_x[section, h] = lax.dot_general(
                left,
                right,
                (((contract,), (contract,)), ((), ())),
                preferred_element_type=jnp.float32,
            ).astype(jnp.bfloat16)
        every_peer(lambda step: x_copies(section, step, start))
        x_own(section)
        gain_t = jnp.broadcast_to(hidden_gain[pl.ds(section, 1), :], (cols, hidden)).T
        shift_t = jnp.broadcast_to(hidden_shift[pl.ds(section, 1), :], (cols, hidden)).T
        bias_t[pl.ds(0, hidden), :] = gain_t
        bias_t[pl.ds(hidden, hidden), :] = shift_t
        wait_all(recv_x.at[section], x_recv_sem.at[section])
        stage[0] = recv_x[section].reshape(hidden * rows, cols).astype(jnp.float32)

        def finish(r, carry):
            values = stage[0, pl.ds(r, hidden, stride=rows), :]
            offset = values - jnp.mean(values, axis=0, keepdims=True)
            spread = jnp.mean(offset * offset, axis=0, keepdims=True)
            normed = offset * lax.rsqrt(spread + HIDDEN_EPSILON) * bias_t[pl.ds(0, hidden), :]
            normed = (normed + bias_t[pl.ds(hidden, hidden), :]).astype(jnp.bfloat16)
            projected = lax.dot_general(
                normed,
                output_weight[section],
                (((0,), (0,)), ((), ())),
                preferred_element_type=jnp.float32,
            )
            out_ref[r] = current[r] + gate[r] * (projected + output_bias[pl.ds(section, 1), :])
            return carry

        lax.fori_loop(0, rows, finish, 0)

    for section in range(2):
        if quarters == 1:
            sent = hidden - per_slot
            for which in range(2):
                wait_all(send_ab.at[section, which, pl.ds(0, sent)], ab_send_sem.at[section, which])
            wait_all(recv_x.at[section, pl.ds(0, sent)], x_send_sem.at[section])
        else:
            every_peer(lambda step: ab_copies(section, step, wait_send))
            every_peer(lambda step: x_copies(section, step, wait_send))


def local(row_total, col_total, pair_rep, residue_mask, *parameters):
    rows, cols, channels = pair_rep.shape
    hidden = parameters[2].shape[2] // 4
    group = hidden // col_total
    per_slot, quarters = (group // row_total, 1) if group >= row_total else (1, row_total // group)
    total = row_total * rows
    part = total // quarters
    sizes = (rows, cols, hidden, row_total, col_total, per_slot, quarters)
    vmem = pl.BlockSpec(memory_space=pltpu.VMEM)
    smem = pl.BlockSpec(memory_space=pltpu.SMEM)
    bf16, f32 = jnp.bfloat16, jnp.float32

    def body(*refs):
        refs = list(refs)
        at = 14 + 5
        recv_a = (refs[at - 1], refs[at])
        merged = refs[: at - 1] + [recv_a] + refs[at + 1 :]
        kernel(sizes, *merged)

    return pl.pallas_call(
        body,
        out_shape=jax.ShapeDtypeStruct((rows, cols, channels), f32),
        in_specs=[vmem, smem] + [vmem] * 11,
        out_specs=vmem,
        scratch_shapes=[
            pltpu.VMEM((4 * hidden, channels), bf16),
            pltpu.VMEM((4 * hidden, cols), f32),
            pltpu.VMEM((2, hidden * rows, cols), f32),
            pltpu.VMEM((2, 2, hidden, rows, cols), bf16),
            pltpu.VMEM((per_slot, part, total), bf16),
            pltpu.VMEM((per_slot, total, part), bf16),
            pltpu.VMEM((2, per_slot, total, total), bf16),
            pltpu.VMEM((2, per_slot, part, total), bf16),
            pltpu.VMEM((2, hidden, rows, cols), bf16),
            pltpu.VMEM((rows, cols, channels), f32),
            pltpu.SemaphoreType.DMA((2, 2)),
            pltpu.SemaphoreType.DMA((2, 2)),
            pltpu.SemaphoreType.DMA((2,)),
            pltpu.SemaphoreType.DMA((2,)),
        ],
        compiler_params=pltpu.CompilerParams(
            collective_id=0, has_side_effects=True, vmem_limit_bytes=48 * 1024 * 1024
        ),
    )(pair_rep, residue_mask, residue_mask.reshape(col_total, cols), *parameters)


def solution(mesh):
    return jax.shard_map(
        functools.partial(local, mesh.shape["row"], mesh.shape["ch"]),
        mesh=mesh,
        in_specs=(P("row", "ch", None), P(), P(), P(), P(), P(), P(), P(), P(), P(), P(), P()),
        out_specs=P("row", "ch", None),
        check_vma=False,
    )
```

time: 240 us -> 111 us (0.46)
  waiting for transfers between devices: 110 us -> 0 us
  Pallas kernels: 0 us -> 100 us
  blocking collectives: 57.4 us -> 0 us
  starting transfers between devices: 39.6 us -> 0 us
  matrix products: 6.89 us -> 0 us
  other arithmetic: 6.83 us -> 0 us
  local copies, waits for them, and re-layouts: 16.7 us -> 10.3 us
    all_to_all x10 -> x0, waiting for transfers between devices: 110 us -> none  [the longest x2 27.6 us: local(): lax.all_to_all(lax.all_to_all(send_left, 'ch', split_axis=0, concat_axis=...]
    pallas_call x0 -> x1, Pallas kernels: none -> 100 us  [local(): pl.pallas_call(body, out_shape=jax.ShapeDtypeStruct((rows, cols, channels...]
    all_to_all x2 -> x0, blocking collectives: 57.4 us -> none  [local(): lax.all_to_all(returned, 'row', split_axis=1, concat_axis=0, tiled=True)]
    all_to_all x10 -> x0, starting transfers between devices: 39.6 us -> none  [the longest x2 9.96 us: local(): lax.all_to_all(lax.all_to_all(send_left, 'ch', split_axis=0, concat_axis=...]
    unnamed x19 -> x25, local copies, waits for them, and re-layouts: 0.93 us -> 10.3 us
    dot_general x8 -> x0, matrix products: 6.89 us -> none  [the longest x2 2.98 us: project(): jnp.einsum('rjc,cf->frj', normed, panel_weight[section_index], preferred_...]
    all_to_all x10 -> x0, local copies, waits for them, and re-layouts: 5.7 us -> none  [the longest x2 2.11 us: local(): lax.all_to_all(returned, 'row', split_axis=1, concat_axis=0, tiled=True)]
    convert_element_type x4 -> x0, local copies, waits for them, and re-layouts: 4.74 us -> none  [the longest x2 2.38 us: project(): left_panel = (cell_mask * jax.nn.sigmoid(features[:hidden_width]) * featu...]
  transfers between devices with their start and end apart: 10 -> 0, of which waited for: 10 -> 0; matrix products, arithmetic and copies ran while one was open for 4% -> 0% of each run, Pallas kernels for 0% -> 0%
where the time goes in v1:
time: 111 us; the launch traced here: 110 us
  Pallas kernels  100 us (90%)
  local copies, waits for them, and re-layouts  10.3 us (9%)
    pallas_call x1, Pallas kernels, local(): pl.pallas_call(body, out_shape=jax.ShapeDtypeStruct((rows, cols, channels...  100 us
    unnamed x25, local copies, waits for them, and re-layouts  10.3 us

profile of v1, /device:TPU:0, one launch (start us, length us, event | category | flops | bytes accessed | tf_op | source)
XLA Modules:
  0.0 110.3 jit_solution(17407197088202409729)
XLA Ops:
  0.0 0.0 copy-start.4
  0.0 0.7 copy-done.4
  0.7 0.0 copy-start
  0.7 1.2 %copy-done = f32[16,128,128]{2,1,0:T(8,128)S(1)} copy-done((f32[16,128,128]{2,1,0:T(8,128)S(1)}, f32[16,128,128]{2,1,0:T(8,128)}, u32[]{:S(2)}) %copy-start) | copy-done | bytes 1048600
  1.9 0.0 copy-start.1
  1.9 0.9 copy-done.1
  2.9 0.0 copy-start.2
  2.9 0.8 copy-done.2
  3.7 0.0 copy-start.3
  3.7 0.8 copy-done.3
  4.5 0.0 copy-start.5
  4.5 0.7 copy-done.5
  5.2 0.0 copy-start.6
  5.2 0.7 copy-done.6
  5.9 0.0 copy-start.7
  5.9 0.7 copy-done.7
  6.6 0.0 copy-start.8
  6.6 0.7 copy-done.8
  7.3 0.0 copy-start.9
  7.3 0.7 copy-done.9
  7.9 0.0 copy-start.10
  7.9 0.7 copy-done.10
  8.6 0.0 copy-start.11
  8.6 0.7 copy-done.11
  9.3 100.0 %shard_map.118 = f32[16,128,128]{2,1,0:T(8,128)S(1)} custom-call(f32[16,128,128]{2,1,0:T(8,128)S(1)} %copy-done, s32[256]{0:T(256)S(1)} %copy-done.4, s32[2,128]{1,0:T(2,128)S(1)} %bitcast.1, f32[2,128]{1,0:T(2,128)S(1)} %copy-done.6, f32[2,128]{1,0:T(2,128)S(1)} %copy-done.7, bf16[2,128,512]{2,1,0:T(8,128)(2,1)S(1)} %copy-done.1, f32[2,512]{1,0:T(2,128)S(1)} %copy-done.5, ...), custom_call_target="tpu_custom_call" | custom-call | tf_op jit(solution)/shard_map/pallas_call | solution.py:269
  109.3 1.0 copy.14
Async XLA Ops:
  0.0 0.7 copy-start.4
  0.7 1.2 %copy-start = (f32[16,128,128]{2,1,0:T(8,128)S(1)}, f32[16,128,128]{2,1,0:T(8,128)}, u32[]{:S(2)}) copy-start(f32[16,128,128]{2,1,0:T(8,128)} %refs_0_.1) | copy-start | bytes 3145732
  1.9 0.9 copy-start.1
  2.9 0.8 copy-start.2
  3.7 0.8 copy-start.3
  4.5 0.7 copy-start.5
  5.2 0.7 copy-start.6
  5.9 0.7 copy-start.7
  6.6 0.7 copy-start.8
  7.3 0.7 copy-start.9
  7.9 0.7 copy-start.10
  8.6 0.7 copy-start.11

commit v2 on v0

v2 whole, which is shorter than its diff:
```python
import functools

import jax
import jax.numpy as jnp
from jax import lax
from jax.experimental import pallas as pl
from jax.experimental.pallas import tpu as pltpu
from jax.sharding import PartitionSpec as P

PAIR_EPSILON = 1e-05
HIDDEN_EPSILON = 1.0
MESH = pl.DeviceIdType.MESH
CHUNKS = 4
NAMES = (
    "pair",
    "mask",
    "pair_gain",
    "pair_shift",
    "panel_weight",
    "panel_bias",
    "gate_weight",
    "gate_bias",
    "hidden_gain",
    "hidden_shift",
    "output_weight",
    "output_bias",
)


def normalize(values, axis, epsilon, gain, shift):
    offset = values - jnp.mean(values, axis=axis, keepdims=True)
    spread = jnp.mean(offset * offset, axis=axis, keepdims=True)
    return (offset * lax.rsqrt(spread + epsilon) * gain + shift).astype(jnp.bfloat16)


def kernel(sizes, mask_smem, *refs):
    rows, cols, hidden, row_total, col_total, parts, chunks = sizes
    count = len(NAMES)
    sources = dict(zip(NAMES, refs[:count]))
    out_ref = refs[count]
    held = dict(zip(NAMES, refs[count + 1 : 2 * count + 1]))
    (
        weight_t,
        bias_t,
        affine_t,
        normed_ref,
        stage,
        stage_x,
        gate,
        send_ab,
        recv_a,
        recv_b,
        recv_ab,
        send_x0,
        send_x1,
        recv_x0,
        recv_x1,
        load_sem,
        a_send_sem,
        a_recv_sem,
        b_send_sem,
        b_recv_sem,
        ab_send_sem,
        ab_recv_sem,
        x_send_sem,
        x_recv_sem,
    ) = refs[2 * count + 1 :]
    devices = row_total * col_total
    row_part = row_total // parts
    members = row_part * col_total
    per_slot = hidden // members
    piece = per_slot // chunks
    wide = hidden // chunks
    total = row_total * rows
    part = total // parts
    my_row = lax.axis_index("row")
    my_col = lax.axis_index("ch")
    my_group = my_row // row_part
    my_place = lax.rem(my_row, row_part) * col_total + my_col

    loads = [
        pltpu.make_async_copy(sources[name], held[name], load_sem.at[at])
        for at, name in enumerate(NAMES)
    ]
    for load in loads:
        load.start()

    def partner(distance, step):
        group = lax.rem(my_group + distance, parts)
        place = lax.rem(my_place + step, members)
        return group * row_part + place // col_total, lax.rem(place, col_total), place

    def each(first, body):
        def step_body(step, carry):
            body(step)
            return carry

        lax.fori_loop(first, members, step_body, 0)

    barrier = pltpu.get_barrier_semaphore()
    for distance in range(parts):

        def greet(step):
            row, col, _ = partner(distance, step)
            pl.semaphore_signal(barrier, inc=1, device_id=(row, col), device_id_type=MESH)

        each(1 if distance == 0 else 0, greet)

    def wait_bytes(ref, sem):
        pltpu.make_async_copy(ref, ref, sem).wait()

    def remote(source, target, send_sem, recv_sem, row, col):
        pltpu.make_async_remote_copy(
            src_ref=source,
            dst_ref=target,
            send_sem=send_sem,
            recv_sem=recv_sem,
            device_id=(row, col),
            device_id_type=MESH,
        ).start()

    row_at = pl.multiple_of(my_row * rows, rows)
    near_at = pl.multiple_of(lax.rem(my_row, row_part) * rows, rows)
    col_at = pl.multiple_of(my_col * cols, cols)

    def panels(chunk, place):
        return pl.ds(chunk * wide + place * piece, piece)

    def send_panels(section, chunk):
        spot = pl.ds(chunk * piece, piece)
        if section == 0:
            a_to = recv_a.at[spot, pl.ds(near_at, rows), pl.ds(col_at, cols)]
            b_to = recv_b.at[spot, pl.ds(row_at, rows), pl.ds(col_at, cols)]

            def far(distance, step):
                row, col, place = partner(distance, step)
                source = send_ab.at[0, 1, panels(chunk, place)]
                remote(
                    source, b_to, b_send_sem.at[distance], b_recv_sem.at[chunk], row, col
                )

            def near(step):
                row, col, place = partner(0, step)
                source = send_ab.at[0, 0, panels(chunk, place)]
                remote(source, a_to, a_send_sem, a_recv_sem.at[chunk], row, col)

            for distance in range(parts - 1, -1, -1):
                each(1 if distance == 0 else 0, functools.partial(far, distance))
            each(1, near)
            own = panels(chunk, my_place)
            pltpu.make_async_copy(send_ab.at[0, 0, own], a_to, a_recv_sem.at[chunk]).start()
            pltpu.make_async_copy(send_ab.at[0, 1, own], b_to, b_recv_sem.at[chunk]).start()
        else:
            to = recv_ab.at[:, spot, pl.ds(near_at, rows), pl.ds(col_at, cols)]

            def both(step):
                row, col, place = partner(0, step)
                source = send_ab.at[1, :, panels(chunk, place)]
                remote(source, to, ab_send_sem, ab_recv_sem.at[chunk], row, col)

            each(1, both)
            own = send_ab.at[1, :, panels(chunk, my_place)]
            pltpu.make_async_copy(own, to, ab_recv_sem.at[chunk]).start()

    def wait_panels(section, chunk):
        spot = pl.ds(chunk * piece, piece)
        if section == 0:
            wait_bytes(recv_a.at[spot], a_recv_sem.at[chunk])
            wait_bytes(recv_b.at[spot], b_recv_sem.at[chunk])
        else:
            wait_bytes(recv_ab.at[:, spot], ab_recv_sem.at[chunk])

    def send_products(section, chunk):
        spot = pl.ds(chunk * piece, piece)
        lands = panels(chunk, my_place)

        def refs_of(row, col):
            to_row = row if section == 1 else lax.rem(row, row_part)
            at = pl.ds(pl.multiple_of(to_row * rows, rows), rows)
            along = pl.ds(pl.multiple_of(col * cols, cols), cols)
            if section == 0:
                return send_x0.at[spot, at, along], recv_x0.at[lands]
            return send_x1.at[spot, at, along], recv_x1.at[my_group, lands]

        def other(distance, step):
            row, col, _ = partner(distance, step)
            source, target = refs_of(row, col)
            remote(
                source,
                target,
                x_send_sem.at[section, distance],
                x_recv_sem.at[section, chunk],
                row,
                col,
            )

        for distance in range(parts - 1 if section == 1 else 0, -1, -1):
            each(1 if distance == 0 else 0, functools.partial(other, distance))
        source, target = refs_of(my_row, my_col)
        pltpu.make_async_copy(source, target, x_recv_sem.at[section, chunk]).start()

    def prepare(section):
        for block in range(4):
            span = slice(block * hidden, (block + 1) * hidden)
            turned = held["panel_weight"][section, :, span].astype(jnp.float32).T
            turned = turned.astype(jnp.bfloat16)
            biases = held["panel_bias"][pl.ds(section, 1), span]
            biases = jnp.broadcast_to(biases, (cols, hidden)).T
            for chunk in range(chunks):
                to = pl.ds((chunk * 4 + block) * wide, wide)
                weight_t[section, to, :] = turned[chunk * wide : (chunk + 1) * wide]
                bias_t[section, to, :] = biases[chunk * wide : (chunk + 1) * wide]
        for at, name in enumerate(("hidden_gain", "hidden_shift")):
            line = held[name][pl.ds(section, 1), :]
            affine_t[section, at] = jnp.broadcast_to(line, (cols, hidden)).T

    def norm_row(section, values):
        return normalize(
            values,
            1,
            PAIR_EPSILON,
            held["pair_gain"][pl.ds(section, 1), :],
            held["pair_shift"][pl.ds(section, 1), :],
        )

    for load in loads:
        load.wait()
    prepare(0)

    def first_norm(r, carry):
        normed_ref[r] = norm_row(0, held["pair"][r])
        return carry

    lax.fori_loop(0, rows, first_norm, 0, unroll=4)
    col_mask = held["mask"][pl.ds(my_col, 1), :].astype(jnp.float32)

    for section in range(2):
        current = held["pair"] if section == 0 else out_ref
        for chunk in range(chunks):

            def project(r, carry):
                span = pl.ds(chunk * 4 * wide, 4 * wide)
                features = lax.dot_general(
                    weight_t[section, span, :],
                    normed_ref[r],
                    (((1,), (1,)), ((), ())),
                    preferred_element_type=jnp.float32,
                )
                features = features + bias_t[section, span, :]
                mask = col_mask * mask_smem[my_row * rows + r].astype(jnp.float32)
                for which in range(2):
                    at = 2 * which * wide
                    panel = mask * jax.nn.sigmoid(features[at : at + wide])
                    panel = panel * features[at + wide : at + 2 * wide]
                    stage[which, pl.ds(r, wide, stride=rows), :] = panel
                return carry

            lax.fori_loop(0, rows, project, 0, unroll=4)
            for which in range(2):
                send_ab[section, which, pl.ds(chunk * wide, wide)] = (
                    stage[which].astype(jnp.bfloat16).reshape(wide, rows, cols)
                )
            if section == 0 and chunk == 0:
                pl.semaphore_wait(barrier, devices - 1)
            send_panels(section, chunk)

        def gates(r, carry):
            gate[r] = jax.nn.sigmoid(
                jnp.dot(
                    normed_ref[r],
                    held["gate_weight"][section],
                    preferred_element_type=jnp.float32,
                )
                + held["gate_bias"][pl.ds(section, 1), :]
            )
            return carry

        lax.fori_loop(0, rows, gates, 0, unroll=4)
        if section == 0:
            prepare(1)
        for chunk in range(chunks):
            wait_panels(section, chunk)
            for h in range(chunk * piece, (chunk + 1) * piece):
                if section == 0:
                    left, right, along, to = recv_a[h], recv_b[h], 1, send_x0
                else:
                    left, right, along, to = recv_ab[0, h], recv_ab[1, h], 0, send_x1
                to[h] = lax.dot_general(
                    left,
                    right,
                    (((along,), (along,)), ((), ())),
                    preferred_element_type=jnp.float32,
                ).astype(jnp.bfloat16)
            send_products(section, chunk)
        for chunk in range(chunks):
            spot = pl.ds(chunk * wide, wide)
            if section == 0:
                wait_bytes(recv_x0.at[spot], x_recv_sem.at[0, chunk])
                got = recv_x0[spot].astype(jnp.float32)
            else:
                wait_bytes(recv_x1.at[:, spot], x_recv_sem.at[1, chunk])
                got = recv_x1[0, spot].astype(jnp.float32)
                for other in range(1, parts):
                    got = got + recv_x1[other, spot].astype(jnp.float32)
            stage_x[pl.ds(chunk * wide * rows, wide * rows), :] = got.reshape(wide * rows, cols)

        def finish(r, carry):
            normed = normalize(
                stage_x[pl.ds(r, hidden, stride=rows), :],
                0,
                HIDDEN_EPSILON,
                affine_t[section, 0],
                affine_t[section, 1],
            )
            projected = lax.dot_general(
                normed,
                held["output_weight"][section],
                (((0,), (0,)), ((), ())),
                preferred_element_type=jnp.float32,
            )
            projected = projected + held["output_bias"][pl.ds(section, 1), :]
            updated = current[r] + gate[r] * projected
            out_ref[r] = updated
            if section == 0:
                normed_ref[r] = norm_row(1, updated)
            return carry

        lax.fori_loop(0, rows, finish, 0, unroll=4)

    one = hidden - per_slot
    wait_bytes(send_ab.at[0, 0, pl.ds(0, one)], a_send_sem)
    wait_bytes(send_ab.at[1, :, pl.ds(0, one)], ab_send_sem)
    for distance in range(parts):
        amount = one if distance == 0 else hidden
        wait_bytes(send_ab.at[0, 1, pl.ds(0, amount)], b_send_sem.at[distance])
        wait_bytes(send_ab.at[0, 1, pl.ds(0, amount)], x_send_sem.at[1, distance])
    wait_bytes(recv_x0.at[pl.ds(0, one)], x_send_sem.at[0, 0])


def local(row_total, col_total, pair_rep, residue_mask, *parameters):
    rows, cols, channels = pair_rep.shape
    hidden = parameters[2].shape[2] // 4
    parts = max(2, row_total * col_total // hidden)
    members = row_total * col_total // parts
    per_slot = hidden // members
    chunks = min(CHUNKS, per_slot)
    wide = hidden // chunks
    total = row_total * rows
    part = total // parts
    sizes = (rows, cols, hidden, row_total, col_total, parts, chunks)
    bf16, f32 = jnp.bfloat16, jnp.float32
    dma = pltpu.SemaphoreType.DMA
    arrays = (pair_rep, residue_mask.reshape(col_total, cols), *parameters)
    return pl.pallas_call(
        functools.partial(kernel, sizes),
        out_shape=jax.ShapeDtypeStruct((rows, cols, channels), f32),
        in_specs=[pl.BlockSpec(memory_space=pltpu.SMEM)]
        + [pl.BlockSpec(memory_space=pltpu.HBM)] * len(arrays),
        out_specs=pl.BlockSpec(memory_space=pltpu.VMEM),
        scratch_shapes=[pltpu.VMEM(array.shape, array.dtype) for array in arrays]
        + [
            pltpu.VMEM((2, 4 * hidden, channels), bf16),
            pltpu.VMEM((2, 4 * hidden, cols), f32),
            pltpu.VMEM((2, 2, hidden, cols), f32),
            pltpu.VMEM((rows, cols, channels), bf16),
            pltpu.VMEM((2, wide * rows, cols), f32),
            pltpu.VMEM((hidden * rows, cols), f32),
            pltpu.VMEM((rows, cols, channels), f32),
            pltpu.VMEM((2, 2, hidden, rows, cols), bf16),
            pltpu.VMEM((per_slot, part, total), bf16),
            pltpu.VMEM((per_slot, total, total), bf16),
            pltpu.VMEM((2, per_slot, part, total), bf16),
            pltpu.VMEM((per_slot, part, total), bf16),
            pltpu.VMEM((per_slot, total, total), bf16),
            pltpu.VMEM((hidden, rows, cols), bf16),
            pltpu.VMEM((parts, hidden, rows, cols), bf16),
            dma((len(arrays),)),
            dma(()),
            dma((chunks,)),
            dma((parts,)),
            dma((chunks,)),
            dma(()),
            dma((chunks,)),
            dma((2, parts)),
            dma((2, chunks)),
        ],
        compiler_params=pltpu.CompilerParams(collective_id=0, has_side_effects=True),
    )(residue_mask, *arrays)


def solution(mesh):
    return jax.shard_map(
        functools.partial(local, mesh.shape["row"], mesh.shape["ch"]),
        mesh=mesh,
        in_specs=(P("row", "ch", None), P(), P(), P(), P(), P(), P(), P(), P(), P(), P(), P()),
        out_specs=P("row", "ch", None),
        check_vma=False,
    )
```

time: 240 us -> 78.2 us (0.33)
  waiting for transfers between devices: 110 us -> 0 us
  Pallas kernels: 0 us -> 75.7 us
  blocking collectives: 57.4 us -> 0 us
  starting transfers between devices: 39.6 us -> 0 us
  local copies, waits for them, and re-layouts: 16.7 us -> 2.3 us
  matrix products: 6.89 us -> 0 us
  other arithmetic: 6.83 us -> 0 us
    all_to_all x10 -> x0, waiting for transfers between devices: 110 us -> none  [the longest x2 27.6 us: local(): lax.all_to_all(lax.all_to_all(send_left, 'ch', split_axis=0, concat_axis=...]
    pallas_call x0 -> x1, Pallas kernels: none -> 75.7 us  [local(): pl.pallas_call(functools.partial(kernel, sizes), out_shape=jax.ShapeDtype...]
    all_to_all x2 -> x0, blocking collectives: 57.4 us -> none  [local(): lax.all_to_all(returned, 'row', split_axis=1, concat_axis=0, tiled=True)]
    all_to_all x10 -> x0, starting transfers between devices: 39.6 us -> none  [the longest x2 9.96 us: local(): lax.all_to_all(lax.all_to_all(send_left, 'ch', split_axis=0, concat_axis=...]
    dot_general x8 -> x0, matrix products: 6.89 us -> none  [the longest x2 2.98 us: project(): jnp.einsum('rjc,cf->frj', normed, panel_weight[section_index], preferred_...]
    all_to_all x10 -> x0, local copies, waits for them, and re-layouts: 5.7 us -> none  [the longest x2 2.11 us: local(): lax.all_to_all(returned, 'row', split_axis=1, concat_axis=0, tiled=True)]
    convert_element_type x4 -> x0, local copies, waits for them, and re-layouts: 4.74 us -> none  [the longest x2 2.38 us: project(): left_panel = (cell_mask * jax.nn.sigmoid(features[:hidden_width]) * featu...]
    reduce_sum x7 -> x0, other arithmetic: 4.14 us -> none  [the longest x4 2.3 us: layer_norm(): spread = jnp.mean(offset * offset, axis=along, keepdims=True)]
  transfers between devices with their start and end apart: 10 -> 0, of which waited for: 10 -> 0; matrix products, arithmetic and copies ran while one was open for 4% -> 0% of each run, Pallas kernels for 0% -> 0%
where the time goes in v2:
time: 78.2 us; the launch traced here: 78 us
  Pallas kernels  75.7 us (97%)
  local copies, waits for them, and re-layouts  2.3 us (3%)
    pallas_call x1, Pallas kernels, local(): pl.pallas_call(functools.partial(kernel, sizes), out_shape=jax.ShapeDtype...  75.7 us
    unnamed x1, local copies, waits for them, and re-layouts  2.3 us

profile of v2, /device:TPU:0, one launch (start us, length us, event | category | flops | bytes accessed | tf_op | source)
XLA Modules:
  0.0 78.0 jit_solution(18044303653536715228)
XLA Ops:
  0.0 75.7 %shard_map.118 = f32[16,128,128]{2,1,0:T(8,128)} custom-call(s32[256]{0:T(256)} %mask_smem.1, f32[16,128,128]{2,1,0:T(8,128)} %refs_0_.1, s32[2,128]{1,0:T(2,128)} %bitcast.1, f32[2,128]{1,0:T(2,128)} %refs_2_.1, f32[2,128]{1,0:T(2,128)} %refs_3_.1, bf16[2,128,512]{2,1,0:T(8,128)(2,1)} %refs_4_.1, f32[2,512]{1,0:T(2,128)} %refs_5_.1, ...), custom_call_target="tpu_custom_call" | custom-call | tf_op jit(solution)/shard_map/pallas_call | solution.py:354
  75.7 2.3 %copy.14 = f32[16,128,128]{2,1,0:T(8,128)} copy(f32[16,128,128]{2,1,0:T(8,128)} %shard_map.118) | data formatting | bytes 2097152

commit v3 on v2

--- a/solution.py
+++ b/solution.py
@@ -11,6 +11,7 @@
 HIDDEN_EPSILON = 1.0
 MESH = pl.DeviceIdType.MESH
 CHUNKS = 4
+LEAD = 3
 NAMES = (
     "pair",
     "mask",
@@ -210,6 +211,8 @@
                 to = pl.ds((chunk * 4 + block) * wide, wide)
                 weight_t[section, to, :] = turned[chunk * wide : (chunk + 1) * wide]
                 bias_t[section, to, :] = biases[chunk * wide : (chunk + 1) * wide]
+
+    def prepare_affine(section):
         for at, name in enumerate(("hidden_gain", "hidden_shift")):
             line = held[name][pl.ds(section, 1), :]
             affine_t[section, at] = jnp.broadcast_to(line, (cols, hidden)).T
@@ -223,20 +226,24 @@
             held["pair_shift"][pl.ds(section, 1), :],
         )
 
-    for load in loads:
-        load.wait()
-    prepare(0)
+    early = [NAMES.index(name) for name in ("pair", "pair_gain", "pair_shift")]
+    for at in early:
+        loads[at].wait()
 
     def first_norm(r, carry):
         normed_ref[r] = norm_row(0, held["pair"][r])
         return carry
 
-    lax.fori_loop(0, rows, first_norm, 0, unroll=4)
+    lax.fori_loop(0, rows, first_norm, 0, unroll=min(rows, 16))
+    for at in range(count):
+        if at not in early:
+            loads[at].wait()
+    prepare(0)
     col_mask = held["mask"][pl.ds(my_col, 1), :].astype(jnp.float32)
 
     for section in range(2):
         current = held["pair"] if section == 0 else out_ref
-        for chunk in range(chunks):
+        def make(chunk):
 
             def project(r, carry):
                 span = pl.ds(chunk * 4 * wide, 4 * wide)
@@ -255,7 +262,7 @@
                     stage[which, pl.ds(r, wide, stride=rows), :] = panel
                 return carry
 
-            lax.fori_loop(0, rows, project, 0, unroll=4)
+            lax.fori_loop(0, rows, project, 0, unroll=min(rows, 16))
             for which in range(2):
                 send_ab[section, which, pl.ds(chunk * wide, wide)] = (
                     stage[which].astype(jnp.bfloat16).reshape(wide, rows, cols)
@@ -275,10 +282,7 @@
             )
             return carry
 
-        lax.fori_loop(0, rows, gates, 0, unroll=4)
-        if section == 0:
-            prepare(1)
-        for chunk in range(chunks):
+        def multiply(chunk):
             wait_panels(section, chunk)
             for h in range(chunk * piece, (chunk + 1) * piece):
                 if section == 0:
@@ -292,6 +296,21 @@
                     preferred_element_type=jnp.float32,
                 ).astype(jnp.bfloat16)
             send_products(section, chunk)
+
+        lead = chunks if section == 0 else min(LEAD, chunks)
+        for chunk in range(lead):
+            make(chunk)
+        if section == 0:
+            lax.fori_loop(0, rows, gates, 0, unroll=min(rows, 16))
+            prepare(1)
+            prepare_affine(0)
+            prepare_affine(1)
+        for chunk in range(chunks):
+            multiply(chunk)
+            if chunk + lead < chunks:
+                make(chunk + lead)
+        if section == 1:
+            lax.fori_loop(0, rows, gates, 0, unroll=min(rows, 16))
         for chunk in range(chunks):
             spot = pl.ds(chunk * wide, wide)
             if section == 0:
@@ -325,7 +344,7 @@
                 normed_ref[r] = norm_row(1, updated)
             return carry
 
-        lax.fori_loop(0, rows, finish, 0, unroll=4)
+        lax.fori_loop(0, rows, finish, 0, unroll=min(rows, 16))
 
     one = hidden - per_slot
     wait_bytes(send_ab.at[0, 0, pl.ds(0, one)], a_send_sem)

time: 78.2 us -> 76.1 us (0.973)
  Pallas kernels: 75.7 us -> 73.6 us
    pallas_call x1, Pallas kernels: 75.7 us -> 73.6 us  [local(): pl.pallas_call(functools.partial(kernel, sizes), out_shape=jax.ShapeDtype...]
where the time goes in v3:
time: 76.1 us; the launch traced here: 75.9 us
  Pallas kernels  73.6 us (97%)
  local copies, waits for them, and re-layouts  2.3 us (3%)
    pallas_call x1, Pallas kernels, local(): pl.pallas_call(functools.partial(kernel, sizes), out_shape=jax.ShapeDtype...  73.6 us
    unnamed x1, local copies, waits for them, and re-layouts  2.3 us

profile of v3, /device:TPU:0, one launch (start us, length us, event | category | flops | bytes accessed | tf_op | source)
XLA Modules:
  0.0 75.9 jit_solution(4474672195709080562)
XLA Ops:
  0.0 73.6 %shard_map.118 = f32[16,128,128]{2,1,0:T(8,128)} custom-call(s32[256]{0:T(256)} %mask_smem.1, f32[16,128,128]{2,1,0:T(8,128)} %refs_0_.1, s32[2,128]{1,0:T(2,128)} %bitcast.1, f32[2,128]{1,0:T(2,128)} %refs_2_.1, f32[2,128]{1,0:T(2,128)} %refs_3_.1, bf16[2,128,512]{2,1,0:T(8,128)(2,1)} %refs_4_.1, f32[2,512]{1,0:T(2,128)} %refs_5_.1, ...), custom_call_target="tpu_custom_call" | custom-call | tf_op jit(solution)/shard_map/pallas_call | solution.py:373
  73.6 2.3 %copy.14 = f32[16,128,128]{2,1,0:T(8,128)} copy(f32[16,128,128]{2,1,0:T(8,128)} %shard_map.118) | data formatting | bytes 2097152

commit v4 on v3

--- a/solution.py
+++ b/solution.py
@@ -96,7 +96,9 @@
             body(step)
             return carry
 
-        lax.fori_loop(first, members, step_body, 0)
+        steps = members - first
+        unroll = max(d for d in (1, 4, 5) if steps % d == 0)
+        lax.fori_loop(first, members, step_body, 0, unroll=unroll)
 
     barrier = pltpu.get_barrier_semaphore()
     for distance in range(parts):

time: 76.1 us -> 75.8 us (level)
  no operation moved by 1% of the time
where the time goes in v4:
time: 75.8 us; the launch traced here: 75.6 us
  Pallas kernels  73.3 us (97%)
  local copies, waits for them, and re-layouts  2.3 us (3%)
    pallas_call x1, Pallas kernels, local(): pl.pallas_call(functools.partial(kernel, sizes), out_shape=jax.ShapeDtype...  73.3 us
    unnamed x1, local copies, waits for them, and re-layouts  2.3 us

profile of v4, /device:TPU:0, one launch (start us, length us, event | category | flops | bytes accessed | tf_op | source)
XLA Modules:
  0.0 75.6 jit_solution(2868536081023350078)
XLA Ops:
  0.0 73.3 %shard_map.118 = f32[16,128,128]{2,1,0:T(8,128)} custom-call(s32[256]{0:T(256)} %mask_smem.1, f32[16,128,128]{2,1,0:T(8,128)} %refs_0_.1, s32[2,128]{1,0:T(2,128)} %bitcast.1, f32[2,128]{1,0:T(2,128)} %refs_2_.1, f32[2,128]{1,0:T(2,128)} %refs_3_.1, bf16[2,128,512]{2,1,0:T(8,128)(2,1)} %refs_4_.1, f32[2,512]{1,0:T(2,128)} %refs_5_.1, ...), custom_call_target="tpu_custom_call" | custom-call | tf_op jit(solution)/shard_map/pallas_call | solution.py:375
  73.3 2.3 %copy.14 = f32[16,128,128]{2,1,0:T(8,128)} copy(f32[16,128,128]{2,1,0:T(8,128)} %shard_map.118) | data formatting | bytes 2097152
